TPU v7x, 1024 devices: a whole 4x4x32 slice. The times are simulated.
1024 devices in a mesh: dp: 2 (over y_hi), ctx: 128 (over z, x), tp: 4 (over y_lo, core).
Axes of the slice: x: 4, y: 4 (y_hi: 2, y_lo: 2; y = y_hi * 2 + y_lo), z: 32, core: 2. Of those that a mesh axis runs over, the one named last changes fastest.
Arguments:
- queries: bfloat16 [4, 16384, 4096], P('dp', 'ctx', 'tp'), may hold values from -6 to 6
- keys: bfloat16 [4, 16384, 512], P('dp', 'ctx', 'tp'), may hold values from -6 to 6
- values: bfloat16 [4, 16384, 512], P('dp', 'ctx', 'tp'), may hold values from -6 to 6
- output_gradient: bfloat16 [4, 16384, 4096], P('dp', 'ctx', 'tp'), may hold values from -6 to 6
- sinks: float32 [64], P('tp'), may hold values from -1 to 3
- doc_starts: int32 [4, 64], P('dp'), may hold values from 0 to 32768, as said below
- valid_counts: int32 [4, 128], P('dp'), may hold values from 64 to 128
Outputs:
- query_grad: bfloat16 [4, 16384, 4096], P('dp', 'ctx', 'tp')
- key_grad: bfloat16 [4, 16384, 512], P('dp', 'ctx', 'tp')
- value_grad: bfloat16 [4, 16384, 512], P('dp', 'ctx', 'tp')
- sink_grad: float32 [64], P('tp')
Inputs may be any that keep to these rules, and one draw needn't show every extreme that they name: `doc_starts`: each row is strictly increasing, begins with 0 and ends with 32768; a start at or past 16384 opens no document.
All inputs are finite; a program needn't handle non-finite values.
Results may differ from a plain program's by a relative error of at most 0.0093.
Values may be sent and summed in bfloat16 or wider, within the bound.
A program may use at most 64 MiB of HBM per device.

v0:
```python
import math

import jax
import jax.numpy as jnp
from jax import lax
from jax.sharding import Mesh
from jax.sharding import PartitionSpec as P

HEAD_DIMENSION = 64
WINDOW_LENGTH = 128
CTX = ("ctx_0", "ctx_1")
DP_CTX = ("dp", "ctx_0", "ctx_1")


masked_score = -1e30


def passed_along(value, axis, steps):
    count = lax.axis_size(axis)
    first, last = (max(0, -steps), min(count, count - steps))
    return lax.ppermute(value, axis, [(source, source + steps) for source in range(first, last)])


def over_axes(value, axes):
    for axis in axes:
        value = lax.psum(value, axis)
    return value


def document_ids(starts, positions):
    return jnp.sum((starts[None, :] <= positions[:, None]).astype(jnp.int32), axis=1)


def key_valid_mask(counts, positions, block_rows):
    block_index = positions // block_rows
    offset = positions - block_index * block_rows
    matches = jnp.arange(counts.shape[0], dtype=jnp.int32)[None, :] == block_index[:, None]
    limits = jnp.sum(jnp.where(matches, counts[None, :], 0), axis=1)
    return offset < limits


def band_grads(
    query_tile_block,
    key_tile_block,
    value_tile_block,
    output_grad_block,
    query_pos,
    key_pos,
    query_doc,
    key_doc,
    key_valid,
    sink_logits,
):
    heads_kv = key_tile_block.shape[2]
    query_group_width = query_tile_block.shape[3]
    scaling = query_tile_block.shape[4] ** (-0.5)
    scores = (
        jnp.einsum(
            "nqhgd,nkhd->nhgqk",
            query_tile_block,
            key_tile_block,
            preferred_element_type=jnp.float32,
        )
        * scaling
    )
    allowed = (key_pos[:, None, :] <= query_pos[:, :, None]) & (
        query_pos[:, :, None] - key_pos[:, None, :] < WINDOW_LENGTH
    )
    allowed = allowed & (query_doc[:, :, None] == key_doc[:, None, :]) & key_valid[:, None, :]
    scores = jnp.where(allowed[:, None, None], scores, masked_score)
    sink_term = sink_logits.reshape(heads_kv, query_group_width)[None, :, :, None]
    maxima = jnp.maximum(jnp.max(scores, axis=-1), sink_term)
    powers = jnp.exp(scores - maxima[..., None])
    sink_exp = jnp.exp(sink_term - maxima)
    denominator = jnp.sum(powers, axis=-1) + sink_exp
    attend = powers / denominator[..., None]
    attend_low = attend.astype(jnp.bfloat16)
    context = jnp.einsum(
        "nhgqk,nkhd->nhgqd", attend_low, value_tile_block, preferred_element_type=jnp.float32
    )
    deltas = jnp.sum(
        jnp.transpose(output_grad_block, (0, 2, 3, 1, 4)).astype(jnp.float32) * context, axis=-1
    )
    grad_attend = jnp.einsum(
        "nqhgd,nkhd->nhgqk", output_grad_block, value_tile_block, preferred_element_type=jnp.float32
    )
    grad_score = attend * (grad_attend - deltas[..., None])
    score_low = grad_score.astype(jnp.bfloat16)
    query_grad = (
        jnp.einsum(
            "nhgqk,nkhd->nqhgd", score_low, key_tile_block, preferred_element_type=jnp.float32
        )
        * scaling
    )
    key_grad = (
        jnp.einsum(
            "nhgqk,nqhgd->nkhd", score_low, query_tile_block, preferred_element_type=jnp.float32
        )
        * scaling
    )
    value_grad = jnp.einsum(
        "nhgqk,nqhgd->nkhd", attend_low, output_grad_block, preferred_element_type=jnp.float32
    )
    sink_grad = -jnp.sum(sink_exp / denominator * deltas, axis=-1)
    return (
        query_grad,
        key_grad,
        value_grad,
        sink_grad.reshape(sink_grad.shape[0], heads_kv * query_group_width),
    )


def blockwise(entries, sink_logits):
    count_all = entries[0].shape[0]
    group_blocks = math.gcd(count_all, max(1, 512 // WINDOW_LENGTH))
    grouped = tuple(
        (
            member.reshape((count_all // group_blocks, group_blocks) + member.shape[1:])
            for member in entries
        )
    )

    def per_group(parts):
        return band_grads(*parts, sink_logits)

    results = lax.map(per_group, grouped)
    return tuple((member.reshape((count_all,) + member.shape[2:]) for member in results))


def block_facts(query_pos, key_pos, doc_starts, valid_counts, block_rows):
    collected = ([], [], [], [], [])
    for sequence_index in range(doc_starts.shape[0]):
        collected[0].append(query_pos)
        collected[1].append(key_pos)
        collected[2].append(
            document_ids(doc_starts[sequence_index], query_pos.reshape(-1)).reshape(query_pos.shape)
        )
        collected[3].append(
            document_ids(doc_starts[sequence_index], key_pos.reshape(-1)).reshape(key_pos.shape)
        )
        collected[4].append(
            key_valid_mask(valid_counts[sequence_index], key_pos.reshape(-1), block_rows).reshape(
                key_pos.shape
            )
        )
    return [jnp.concatenate(member, axis=0) for member in collected]


def local(queries, keys, values, output_gradient, sinks, doc_starts, valid_counts):
    seq_count, row_count, query_width = queries.shape
    kv_width = keys.shape[2]
    heads_kv = kv_width // HEAD_DIMENSION
    query_group_width = sinks.shape[0] // heads_kv
    block_tiles = row_count // WINDOW_LENGTH
    start_pos = lax.axis_index(CTX) * row_count
    halo_tails = passed_along((keys, values), CTX, 1)

    def pair_rows(extended):
        shaped = extended.reshape(
            seq_count, block_tiles + 1, WINDOW_LENGTH, heads_kv, HEAD_DIMENSION
        )
        joined = jnp.concatenate([shaped[:, :-1], shaped[:, 1:]], axis=2)
        return joined.reshape(seq_count * block_tiles, 2 * WINDOW_LENGTH, heads_kv, HEAD_DIMENSION)

    query_lines = start_pos + jnp.arange(row_count, dtype=jnp.int32).reshape(
        block_tiles, WINDOW_LENGTH
    )
    key_lines = (
        start_pos - WINDOW_LENGTH + jnp.arange(row_count + WINDOW_LENGTH, dtype=jnp.int32)
    ).reshape(block_tiles + 1, WINDOW_LENGTH)
    key_lines = jnp.concatenate([key_lines[:-1], key_lines[1:]], axis=1)
    entries = [
        queries.reshape(
            seq_count * block_tiles, WINDOW_LENGTH, heads_kv, query_group_width, HEAD_DIMENSION
        ),
        pair_rows(jnp.concatenate([halo_tails[0], keys], axis=1)),
        pair_rows(jnp.concatenate([halo_tails[1], values], axis=1)),
        output_gradient.reshape(
            seq_count * block_tiles, WINDOW_LENGTH, heads_kv, query_group_width, HEAD_DIMENSION
        ),
    ] + block_facts(query_lines, key_lines, doc_starts, valid_counts, row_count)
    main_count = seq_count * block_tiles
    dq_all, dk_all, dv_all, sink_part = blockwise(entries, sinks)
    dk_main = dk_all.reshape(seq_count, block_tiles, 2 * WINDOW_LENGTH, kv_width)
    dv_main = dv_all.reshape(seq_count, block_tiles, 2 * WINDOW_LENGTH, kv_width)
    edge_keys, edge_values = (
        passed_along(dk_main[:, 0, :WINDOW_LENGTH].astype(jnp.bfloat16), CTX, -1).astype(
            jnp.float32
        ),
        passed_along(dv_main[:, 0, :WINDOW_LENGTH].astype(jnp.bfloat16), CTX, -1).astype(
            jnp.float32
        ),
    )
    key_total = dk_main[:, :, WINDOW_LENGTH:] + jnp.concatenate(
        [dk_main[:, 1:, :WINDOW_LENGTH], edge_keys[:, None]], axis=1
    )
    value_total = dv_main[:, :, WINDOW_LENGTH:] + jnp.concatenate(
        [dv_main[:, 1:, :WINDOW_LENGTH], edge_values[:, None]], axis=1
    )
    query_grad = dq_all.reshape(seq_count, row_count, query_width).astype(jnp.bfloat16)
    key_grad = key_total.reshape(seq_count, row_count, kv_width).astype(jnp.bfloat16)
    value_grad = value_total.reshape(seq_count, row_count, kv_width).astype(jnp.bfloat16)
    sink_grad = over_axes(jnp.sum(sink_part, axis=0), DP_CTX)
    return (query_grad, key_grad, value_grad, sink_grad)


def solution(mesh):
    torus = Mesh(
        mesh.devices.reshape(mesh.shape["dp"], 32, 4, mesh.shape["tp"]),
        ("dp", "ctx_0", "ctx_1", "tp"),
    )
    placed = (
        P("dp", CTX, "tp"),
        P("dp", CTX, "tp"),
        P("dp", CTX, "tp"),
        P("dp", CTX, "tp"),
        P("tp"),
        P("dp", None),
        P("dp", None),
    )
    return jax.shard_map(
        local,
        mesh=torus,
        in_specs=placed,
        out_specs=(P("dp", CTX, "tp"), P("dp", CTX, "tp"), P("dp", CTX, "tp"), P("tp")),
        check_vma=False,
    )
```

profile of v0, /device:TPU:24, one launch (start us, length us, event | category | flops | bytes accessed | tf_op | source)
XLA Modules:
  0.0 120.5 jit_solution(14875904744860015523)
XLA Ops:
  0.6 3.4 %collective-permute-start = (bf16[2,128,128]{2,1,0:T(8,128)(2,1)}, bf16[2,128,128]{2,1,0:T(8,128)(2,1)S(1)}, u32[]{:S(2)}, u32[]{:S(2)}) collective-permute-start(bf16[2,128,128]{2,1,0:T(8,128)(2,1)} %param.8), channel_id=1, source_target_pairs={{0,4},{4,8},{8,12},{12,16},{16,20},{20,24},{24,28},{28,32},{32,36}... | collective-permute-start | bytes 196616 | tf_op jit(solution)/shard_map/ppermute | solution.py:21
  4.0 3.4 %collective-permute-start.1 = (bf16[2,128,128]{2,1,0:T(8,128)(2,1)}, bf16[2,128,128]{2,1,0:T(8,128)(2,1)S(1)}, u32[]{:S(2)}, u32[]{:S(2)}) collective-permute-start(bf16[2,128,128]{2,1,0:T(8,128)(2,1)} %param.9), channel_id=1, source_target_pairs={{0,4},{4,8},{8,12},{12,16},{16,20},{20,24},{24,28},{28,32},{32,36}... | collective-permute-start | bytes 196616 | tf_op jit(solution)/shard_map/ppermute | solution.py:21
  7.5 0.8 slice_bitcast_fusion
  8.3 0.2 select_reduce_fusion.1
  8.5 0.8 slice_bitcast_fusion.2
  9.3 0.1 convert_reduce_fusion.1
  9.4 0.1 convert_reduce_fusion.3
  9.6 0.3 fusion.13
  9.8 1.3 %copy.43 = bf16[2,128,1024]{1,2,0:T(8,128)(2,1)S(1)} copy(bf16[2,128,1024]{2,1,0:T(8,128)(2,1)} %param.7) | data formatting | bytes 1048576 | tf_op args[0]
  11.2 0.7 max.21
  11.9 1.3 %copy.47 = bf16[2,128,1024]{1,2,0:T(8,128)(2,1)S(1)} copy(bf16[2,128,1024]{2,1,0:T(8,128)(2,1)} %param.10) | data formatting | bytes 1048576 | tf_op args[3]
  13.2 0.0 collective-permute-done
  13.2 0.9 pad_maximum_fusion
  14.1 0.1 reshape.371
  14.2 0.2 fusion.27
  14.4 0.1 copy.69
  14.5 0.1 copy.70
  14.6 0.8 fusion.4
  15.4 0.1 broadcast_maximum_fusion
  15.5 1.0 fusion.3
  16.4 0.1 fusion.19
  16.5 0.0 copy-start.2
  16.5 1.3 %fusion.8 = f32[2,2,256,64,1]{2,3,4,1,0:T(8,128)S(1)} fusion(bf16[2,128,2,8,64]{1,4,3,2,0:T(8,128)(2,1)S(1)} %bitcast.105, f32[2,2,256,128,8]{3,2,4,1,0:T(8,128)S(1)} %get-tuple-element.80, f32[2,2,8,128]{3,2,1,0:T(8,128)S(1)} %fusion.19, f32[2,2,8,128]{3,2,1,0:T(8,128)S(1)} %broadcast_maximum_fusion, pred[2,128,256]{1,2,0:T(8,128)(4,1)S(1)} %fusion.13), kind=kOutput, calls=%fused_computation.14 | convolution fusion | flops 139460608 | bytes 5079040 | tf_op jit(solution)/shard_map/while/body/eval_jaxpr/nhgqk,nqhgd->nkhd/dot_general | solution.py:101
  17.9 0.0 collective-permute-done.1
  17.9 0.1 reshape.372
  18.1 0.2 fusion.28
  18.2 0.1 copy.71
  18.3 0.1 copy.72
  18.5 3.6 %fusion.6 = f32[2,2,8,128]{3,2,1,0:T(8,128)S(1)} fusion(bf16[2,128,2,8,64]{1,4,3,2,0:T(8,128)(2,1)S(1)} %bitcast.106, bf16[2,1,128,2,64]{2,4,3,0,1:T(8,128)(2,1)S(1)} %copy.72, bf16[2,1,128,2,64]{2,4,3,0,1:T(8,128)(2,1)S(1)} %copy.71, f32[2,2,256,128,8]{3,2,4,1,0:T(8,128)} %copy-done, f32[2,2,8,128]{3,2,1,0:T(8,128)S(1)} %fusion.19, ...), kind=kOutput, calls=%fused_computation.11 | convolution fusion | flops 140505088 | bytes 4964352 | tf_op jit(solution)/shard_map/while/body/eval_jaxpr/nhgqk,nkhd->nhgqd/dot_general | solution.py:78
  22.1 1.5 %fusion.1 = bf16[2,2,8,128,256]{3,4,2,1,0:T(8,128)(2,1)S(1)} fusion(bf16[2,128,2,8,64]{1,4,3,2,0:T(8,128)(2,1)S(1)} %bitcast.107, f32[2,2,8,128]{3,2,1,0:T(8,128)S(1)} %fusion.6, bf16[2,1,128,2,64]{2,4,3,0,1:T(8,128)(2,1)S(1)} %copy.72, bf16[2,1,128,2,64]{2,4,3,0,1:T(8,128)(2,1)S(1)} %copy.71, f32[2,2,8,128]{3,2,1,0:T(8,128)S(1)} %fusion.19, ...), kind=kOutput, calls=%fused_computation.2 | convolution fusion | flops 141819904 | bytes 7061504 | tf_op jit(solution)/shard_map/while/body/eval_jaxpr/nqhgd,nkhd->nhgqk/dot_general | solution.py:84
  23.5 0.8 fusion.7
  24.3 0.5 fusion.5
  24.8 0.1 copy.76
  24.9 1.3 %collective-permute-start.3 = (bf16[2,128,128]{2,1,0:T(8,128)(2,1)S(1)}, bf16[2,128,128]{2,1,0:T(8,128)(2,1)S(1)}, u32[]{:S(2)}, u32[]{:S(2)}) collective-permute-start(bf16[2,128,128]{2,1,0:T(8,128)(2,1)S(1)} %bitcast.110), channel_id=1, source_target_pairs={{4,0},{8,4},{12,8},{16,12},{20,16},{24,20},{28,24},{32,28},{36,32}... | collective-permute-start | bytes 196616 | tf_op jit(solution)/shard_map/ppermute | solution.py:21
  26.2 0.2 multiply_reduce_fusion
  26.4 0.1 neg.9
  26.5 0.1 copy.75
  26.6 0.1 copy.73
  26.7 0.1 copy.74
  26.8 1.3 %collective-permute-start.2 = (bf16[2,128,128]{2,1,0:T(8,128)(2,1)S(1)}, bf16[2,128,128]{2,1,0:T(8,128)(2,1)S(1)}, u32[]{:S(2)}, u32[]{:S(2)}) collective-permute-start(bf16[2,128,128]{2,1,0:T(8,128)(2,1)S(1)} %bitcast.111), channel_id=1, source_target_pairs={{4,0},{8,4},{12,8},{16,12},{20,16},{24,20},{28,24},{32,28},{36,32}... | collective-permute-start | bytes 196616 | tf_op jit(solution)/shard_map/ppermute | solution.py:21
  28.1 1.0 copy.56
  29.1 6.4 %psum.21 = f32[16]{0:T(128)S(1)} all-reduce(f32[16]{0:T(128)S(1)} %neg.9), channel_id=1, replica_groups=mesh['dp'=2,'ctx_0'=32,'ctx_1'=4,'tp'=4] {'dp'}, use_global_device_ids=true, to_apply=%region_10.11 | all-reduce | flops 16 | bytes 128 | tf_op jit(solution)/shard_map/psum | solution.py:26
  35.6 73.9 %psum.22 = f32[16]{0:T(128)S(1)} all-reduce(f32[16]{0:T(128)S(1)} %psum.21), channel_id=1, replica_groups=mesh['dp'=2,'ctx_0'=32,'ctx_1'=4,'tp'=4] {'ctx_0'}, use_global_device_ids=true, to_apply=%region_11.12 | all-reduce | flops 16 | bytes 128 | tf_op jit(solution)/shard_map/psum | solution.py:26
  109.5 9.7 %psum.23 = f32[16]{0:T(128)} all-reduce(f32[16]{0:T(128)S(1)} %psum.22), channel_id=1, replica_groups=mesh['dp'=2,'ctx_0'=32,'ctx_1'=4,'tp'=4] {'ctx_1'}, use_global_device_ids=true, to_apply=%region_12.13 | all-reduce | flops 16 | bytes 128 | tf_op jit(solution)/shard_map/psum | solution.py:26
  119.2 0.0 collective-permute-done.3
  119.2 0.6 fusion.18
  119.8 0.0 collective-permute-done.2
  119.8 0.6 fusion.17
  (22 shorter events, 0.2 us)
Async XLA Ops:
  0.6 12.6 %collective-permute-start = (bf16[2,128,128]{2,1,0:T(8,128)(2,1)}, bf16[2,128,128]{2,1,0:T(8,128)(2,1)S(1)}, u32[]{:S(2)}, u32[]{:S(2)}) collective-permute-start(bf16[2,128,128]{2,1,0:T(8,128)(2,1)} %param.8), channel_id=1, source_target_pairs={{0,4},{4,8},{8,12},{12,16},{16,20},{20,24},{24,28},{28,32},{32,36}... | collective-permute-start | bytes 196616 | tf_op jit(solution)/shard_map/ppermute | solution.py:21
  4.0 13.8 %collective-permute-start.1 = (bf16[2,128,128]{2,1,0:T(8,128)(2,1)}, bf16[2,128,128]{2,1,0:T(8,128)(2,1)S(1)}, u32[]{:S(2)}, u32[]{:S(2)}) collective-permute-start(bf16[2,128,128]{2,1,0:T(8,128)(2,1)} %param.9), channel_id=1, source_target_pairs={{0,4},{4,8},{8,12},{12,16},{16,20},{20,24},{24,28},{28,32},{32,36}... | collective-permute-start | bytes 196616 | tf_op jit(solution)/shard_map/ppermute | solution.py:21
  15.4 2.4 %copy-start = (f32[2,2,256,128,8]{3,2,4,1,0:T(8,128)}, f32[2,2,256,128,8]{3,2,4,1,0:T(8,128)S(1)}, u32[]{:S(2)}) copy-start(f32[2,2,256,128,8]{3,2,4,1,0:T(8,128)S(1)} %get-tuple-element.80) | copy-start | bytes 12582916
  16.5 1.4 %copy-start.2 = (bf16[2,128,128]{2,1,0:T(8,128)(2,1)S(1)}, bf16[2,128,128]{2,1,0:T(8,128)(2,1)}, u32[]{:S(2)}) copy-start(bf16[2,128,128]{2,1,0:T(8,128)(2,1)} %param.9) | copy-start | bytes 196612
  18.5 3.6 %copy-start.1 = (f32[2,2,256,128,8]{3,2,4,1,0:T(8,128)S(1)}, f32[2,2,256,128,8]{3,2,4,1,0:T(8,128)}, u32[]{:S(2)}) copy-start(f32[2,2,256,128,8]{3,2,4,1,0:T(8,128)} %copy-done) | copy-start | bytes 12582916
  24.9 94.2 %collective-permute-start.3 = (bf16[2,128,128]{2,1,0:T(8,128)(2,1)S(1)}, bf16[2,128,128]{2,1,0:T(8,128)(2,1)S(1)}, u32[]{:S(2)}, u32[]{:S(2)}) collective-permute-start(bf16[2,128,128]{2,1,0:T(8,128)(2,1)S(1)} %bitcast.110), channel_id=1, source_target_pairs={{4,0},{8,4},{12,8},{16,12},{20,16},{24,20},{28,24},{32,28},{36,32}... | collective-permute-start | bytes 196616 | tf_op jit(solution)/shard_map/ppermute | solution.py:21
  26.8 93.0 %collective-permute-start.2 = (bf16[2,128,128]{2,1,0:T(8,128)(2,1)S(1)}, bf16[2,128,128]{2,1,0:T(8,128)(2,1)S(1)}, u32[]{:S(2)}, u32[]{:S(2)}) collective-permute-start(bf16[2,128,128]{2,1,0:T(8,128)(2,1)S(1)} %bitcast.111), channel_id=1, source_target_pairs={{4,0},{8,4},{12,8},{16,12},{20,16},{24,20},{28,24},{32,28},{36,32}... | collective-permute-start | bytes 196616 | tf_op jit(solution)/shard_map/ppermute | solution.py:21
where the time goes:
time: 121 us; the launch traced here: 120 us
  blocking collectives  90 us (74%)
  starting transfers between devices  9.39 us (8%)
  matrix products  8.31 us (7%)
  local copies, waits for them, and re-layouts  7.51 us (6%)
  other arithmetic  4.22 us (3%)
    psum x3, blocking collectives, over_axes(): value = lax.psum(value, axis)  90 us
    ppermute x4, starting transfers between devices, passed_along(): lax.ppermute(value, axis, [(source, source + steps) for source in range(f...  9.39 us
    unnamed x17, local copies, waits for them, and re-layouts  4.48 us
    dot_general x1, matrix products, band_grads(): jnp.einsum('nhgqk,nkhd->nhgqd', attend_low, value_tile_block, preferred_e...  3.57 us
  transfers between devices with their start and end apart: 4, of which 0 were waited for; matrix products, arithmetic and copies ran while one was open for 10% of the time, Pallas kernels for 0%

commit v1 on v0

v1 whole, which is shorter than its diff:
```python
import functools

import jax
import jax.numpy as jnp
from jax import lax
from jax.experimental import pallas as pl
from jax.experimental.pallas import tpu as pltpu
from jax.sharding import PartitionSpec as P

MESH = pl.DeviceIdType.MESH
BF16 = jnp.bfloat16
F32 = jnp.float32
T = 128
D = 64
LANES = 128
LOG2E = 1.4426950408889634
MASKED = -1e30
NX = 4


def nt(a, b):
    return lax.dot_general(a, b, (((1,), (1,)), ((), ())), preferred_element_type=F32)


def nn(a, b):
    return jnp.dot(a, b, preferred_element_type=F32)


def swap_halves(x):
    return jnp.concatenate([x[:, D:], x[:, :D]], axis=1)


def kernel(
    nz,
    ndp,
    n_seq,
    n_head,
    q_hbm,
    k_hbm,
    v_hbm,
    g_hbm,
    sinks_hbm,
    starts_hbm,
    counts_hbm,
    dq_out,
    dk_out,
    dv_out,
    sink_out,
    q,
    g,
    kv_own,
    kv_prev,
    sinks,
    starts,
    counts,
    qs,
    gs,
    kt,
    bias,
    s_own,
    p_own,
    e_buf,
    p_buf,
    stats,
    sink_acc,
    plane,
    ring,
    dkv_own,
    dkv_send,
    dkv_recv,
    dq_v,
    dkv_v,
    in_sem,
    out_sem,
    halo_send,
    halo_recv,
    grad_send,
    grad_recv,
    plane_send,
    plane_recv,
    ring_send,
    ring_recv,
):
    n_ctx = nz * NX
    ctx = lax.axis_index("ctx")
    dp = lax.axis_index("dp")
    z = ctx // NX
    x = ctx % NX
    right = (ctx + 1) % n_ctx
    left = (ctx + n_ctx - 1) % n_ctx
    n_plane = NX * ndp
    my_plane = dp * NX + x

    def plane_peer(k):
        other = (my_plane + k) % n_plane
        return {"ctx": z * NX + other % NX, "dp": other // NX}

    def ring_peer(k):
        return {"ctx": ((z + k) % nz) * NX + x}

    barrier = pltpu.get_barrier_semaphore()
    pl.semaphore_signal(barrier, inc=1, device_id={"ctx": left}, device_id_type=MESH)
    pl.semaphore_signal(barrier, inc=1, device_id={"ctx": right}, device_id_type=MESH)
    for k in range(1, n_plane):
        pl.semaphore_signal(barrier, inc=1, device_id=plane_peer(k), device_id_type=MESH)
    for k in range(1, nz):
        pl.semaphore_signal(barrier, inc=1, device_id=ring_peer(k), device_id_type=MESH)

    loads = [
        pltpu.make_async_copy(k_hbm, kv_own.at[0], in_sem.at[0]),
        pltpu.make_async_copy(v_hbm, kv_own.at[1], in_sem.at[1]),
        pltpu.make_async_copy(starts_hbm, starts, in_sem.at[2]),
        pltpu.make_async_copy(counts_hbm, counts, in_sem.at[3]),
        pltpu.make_async_copy(sinks_hbm, sinks, in_sem.at[4]),
        pltpu.make_async_copy(q_hbm, q, in_sem.at[5]),
        pltpu.make_async_copy(g_hbm, g, in_sem.at[6]),
    ]
    for copy in loads:
        copy.start()
    loads[0].wait()
    loads[1].wait()
    pl.semaphore_wait(barrier, 2 + (n_plane - 1) + (nz - 1))

    halos = []
    for b in range(n_seq):
        for t in range(2):
            copy = pltpu.make_async_remote_copy(
                src_ref=kv_own.at[t, b],
                dst_ref=kv_prev.at[t, b],
                send_sem=halo_send.at[2 * b + t],
                recv_sem=halo_recv.at[2 * b + t],
                device_id={"ctx": right},
                device_id_type=MESH,
            )
            copy.start()
            halos.append(copy)

    key_row = lax.broadcasted_iota(jnp.int32, (T, T), 0)
    query_col = lax.broadcasted_iota(jnp.int32, (T, T), 1)
    own_slot = key_row <= query_col
    lane = lax.broadcasted_iota(jnp.int32, (8, T), 1)
    pos_own = ctx * T + lane
    pos_prev = pos_own - T
    loads[2].wait()
    loads[3].wait()
    loads[4].wait()
    for b in range(n_seq):
        id_own = jnp.zeros((8, T), jnp.int32)
        id_prev = jnp.zeros((8, T), jnp.int32)
        for i in range(starts.shape[1]):
            start = starts[b, i]
            id_own += jnp.where(pos_own >= start, 1, 0)
            id_prev += jnp.where(pos_prev >= start, 1, 0)
        own_f = jnp.broadcast_to(id_own.astype(F32)[0:1], (T, T))
        prev_f = jnp.broadcast_to(id_prev.astype(F32)[0:1], (T, T))
        key_f = jnp.where(own_slot, own_f.T, prev_f.T)
        limit = jnp.where(own_slot, counts[b, ctx], jnp.where(ctx > 0, counts[b, left], 0))
        bias[b] = jnp.where((key_f == own_f) & (key_row < limit), 0.0, MASKED)

    loads[5].wait()
    loads[6].wait()
    low = lax.broadcasted_iota(jnp.int32, (T, LANES), 1) < D
    heads_per_kv = n_head // 2
    for b in range(n_seq):
        for src, dst in ((q, qs), (g, gs)):
            for pair in range(n_head // 2):
                block = src[b, :, pair * LANES : (pair + 1) * LANES]
                swapped = swap_halves(block)
                first_kv = 2 * pair < heads_per_kv
                even, odd = (block, swapped) if first_kv else (swapped, block)
                keep = low if first_kv else jnp.logical_not(low)
                zero = jnp.zeros_like(block)
                dst[b, (2 * pair) * T : (2 * pair + 1) * T, :] = jnp.where(keep, even, zero)
                dst[b, (2 * pair + 1) * T : (2 * pair + 2) * T, :] = jnp.where(keep, odd, zero)

    W = 2 * T
    n_chunk = n_head * T // W
    for b in range(n_seq):
        for c in range(n_chunk):
            cols = slice(c * W, (c + 1) * W)
            s_own[b, :, cols] = nt(kv_own[0, b], qs[b, cols, :])
            p_own[b, :, cols] = nt(kv_own[1, b], gs[b, cols, :])

    scale = D**-0.5
    own2 = lax.broadcasted_iota(jnp.int32, (T, W), 0) <= (
        lax.broadcasted_iota(jnp.int32, (T, W), 1) % T
    )
    for b in range(n_seq):
        halos[2 * b].wait_recv()
        halos[2 * b + 1].wait_recv()
        for c in range(n_chunk):
            cols = slice(c * W, (c + 1) * W)
            s_prev = nt(kv_prev[0, b], qs[b, cols, :])
            p_prev = nt(kv_prev[1, b], gs[b, cols, :])
            s = jnp.where(own2, s_own[b, :, cols], s_prev) * scale
            s = s + jnp.concatenate([bias[b], bias[b]], axis=1)
            dprob = jnp.where(own2, p_own[b, :, cols], p_prev)
            sink = jnp.concatenate(
                [jnp.full((1, T), sinks[2 * c], F32), jnp.full((1, T), sinks[2 * c + 1], F32)],
                axis=1,
            )
            top = jnp.maximum(jnp.max(s, axis=0, keepdims=True), sink)
            e = jnp.exp(s - top)
            sink_e = jnp.exp(sink - top)
            den = jnp.sum(e, axis=0, keepdims=True) + sink_e
            inv = 1.0 / den
            delta = jnp.sum(e * dprob, axis=0, keepdims=True) * inv
            e_buf[b, :, cols] = e
            p_buf[b, :, cols] = dprob
            stats[b, 0:1, cols] = inv
            stats[b, 1:2, cols] = delta
            part = sink_e * inv * delta
            for i in range(2):
                row = part[:, i * T : (i + 1) * T]
                h = 2 * c + i
                if b == 0:
                    sink_acc[h : h + 1, :] = row
                else:
                    sink_acc[h : h + 1, :] = sink_acc[h : h + 1, :] + row

    per_head = jnp.sum(sink_acc[...], axis=1, keepdims=True)
    pick = lax.broadcasted_iota(jnp.int32, (n_head, LANES), 0) == lax.broadcasted_iota(
        jnp.int32, (n_head, LANES), 1
    )
    row = jnp.sum(jnp.where(pick, per_head, 0.0), axis=0, keepdims=True)
    plane[pl.ds(my_plane, 1), :] = row

    plane_copies = []
    for k in range(1, n_plane):
        copy = pltpu.make_async_remote_copy(
            src_ref=plane.at[pl.ds(my_plane, 1)],
            dst_ref=plane.at[pl.ds(my_plane, 1)],
            send_sem=plane_send.at[k],
            recv_sem=plane_recv.at[k],
            device_id=plane_peer(k),
            device_id_type=MESH,
        )
        copy.start()
        plane_copies.append(copy)

    ring_copies = []
    grad_copies = []
    out_copies = []

    def backward(b):
        k_all = jnp.concatenate([kv_own[0, b], kv_prev[0, b]], axis=0)
        kt[...] = k_all.T
        dk = jnp.zeros((2 * T, LANES), F32)
        dv = jnp.zeros((2 * T, LANES), F32)
        for c in range(n_chunk):
            cols = slice(c * W, (c + 1) * W)
            p = e_buf[b, :, cols] * stats[b, 0:1, cols]
            ds = p * (p_buf[b, :, cols] - stats[b, 1:2, cols])
            zero = jnp.zeros_like(p)
            p_low = jnp.concatenate(
                [jnp.where(own2, p, zero).astype(BF16), jnp.where(own2, zero, p).astype(BF16)],
                axis=0,
            )
            ds_low = jnp.concatenate(
                [jnp.where(own2, ds, zero).astype(BF16), jnp.where(own2, zero, ds).astype(BF16)],
                axis=0,
            )
            dv += nn(p_low, gs[b, cols, :])
            dk += nn(ds_low, qs[b, cols, :])
            dqt = nn(kt[...], ds_low)
            kv = 0 if 2 * c < heads_per_kv else 1
            part = dqt[kv * D : (kv + 1) * D, :]
            pair = jnp.concatenate([part[:, :T], part[:, T:]], axis=0)
            dq_v[b, :, c * LANES : (c + 1) * LANES] = (pair.T * scale).astype(BF16)
        dk = dk * scale
        dkv_own[0, b] = dk[:T]
        dkv_own[1, b] = dv[:T]
        dkv_send[0, b] = dk[T:].astype(BF16)
        dkv_send[1, b] = dv[T:].astype(BF16)
        copy = pltpu.make_async_copy(dq_v.at[b], dq_out.at[b], out_sem.at[b])
        copy.start()
        out_copies.append(copy)

    backward(0)
    for copy in plane_copies:
        copy.wait_recv()
    ring[pl.ds(z, 1), :] = jnp.sum(plane[...], axis=0, keepdims=True)
    order = sorted(range(1, nz), key=lambda k: -min(k, nz - k))
    for k in order:
        copy = pltpu.make_async_remote_copy(
            src_ref=ring.at[pl.ds(z, 1)],
            dst_ref=ring.at[pl.ds(z, 1)],
            send_sem=ring_send.at[k],
            recv_sem=ring_recv.at[k],
            device_id=ring_peer(k),
            device_id_type=MESH,
        )
        copy.start()
        ring_copies.append(copy)
    for b in range(1, n_seq):
        backward(b)
    for t in range(2):
        copy = pltpu.make_async_remote_copy(
            src_ref=dkv_send.at[t],
            dst_ref=dkv_recv.at[t],
            send_sem=grad_send.at[t],
            recv_sem=grad_recv.at[t],
            device_id={"ctx": left},
            device_id_type=MESH,
        )
        copy.start()
        grad_copies.append(copy)
    not_last = jnp.where(ctx < n_ctx - 1, 1.0, 0.0)
    for t, out in ((0, dk_out), (1, dv_out)):
        grad_copies[t].wait_recv()
        dkv_v[t] = (dkv_own[t] + dkv_recv[t].astype(F32) * not_last).astype(BF16)
        copy = pltpu.make_async_copy(dkv_v.at[t], out, out_sem.at[n_seq + t])
        copy.start()
        out_copies.append(copy)
    for copy in halos + plane_copies + ring_copies + grad_copies:
        copy.wait_send()
    for copy in out_copies:
        copy.wait()
    for copy in ring_copies:
        copy.wait_recv()
    sink_out[...] = -jnp.sum(ring[...], axis=0, keepdims=True)[:, :n_head]


def solution(mesh):
    n_ctx, ndp, ntp = mesh.shape["ctx"], mesh.shape["dp"], mesh.shape["tp"]
    nz = n_ctx // NX

    def local(queries, keys, values, output_gradient, sinks, doc_starts, valid_counts):
        n_seq, rows, q_width = queries.shape
        n_head = sinks.shape[0]
        kv_width = keys.shape[2]
        any_space = pl.BlockSpec(memory_space=pl.ANY)
        cols = n_head * T
        outs = pl.pallas_call(
            functools.partial(kernel, nz, ndp, n_seq, n_head),
            out_shape=(
                jax.ShapeDtypeStruct(queries.shape, BF16),
                jax.ShapeDtypeStruct(keys.shape, BF16),
                jax.ShapeDtypeStruct(values.shape, BF16),
                jax.ShapeDtypeStruct((1, n_head), F32),
            ),
            in_specs=[any_space] * 7,
            out_specs=(
                any_space,
                any_space,
                any_space,
                pl.BlockSpec(memory_space=pltpu.VMEM),
            ),
            scratch_shapes=[
                pltpu.VMEM((n_seq, rows, q_width), BF16),
                pltpu.VMEM((n_seq, rows, q_width), BF16),
                pltpu.VMEM((2, n_seq, rows, kv_width), BF16),
                pltpu.VMEM((2, n_seq, rows, kv_width), BF16),
                pltpu.SMEM((n_head,), F32),
                pltpu.SMEM(doc_starts.shape, jnp.int32),
                pltpu.SMEM(valid_counts.shape, jnp.int32),
                pltpu.VMEM((n_seq, cols, LANES), BF16),
                pltpu.VMEM((n_seq, cols, LANES), BF16),
                pltpu.VMEM((LANES, 2 * T), BF16),
                pltpu.VMEM((n_seq, T, T), F32),
                pltpu.VMEM((n_seq, T, cols), F32),
                pltpu.VMEM((n_seq, T, cols), F32),
                pltpu.VMEM((n_seq, T, cols), F32),
                pltpu.VMEM((n_seq, T, cols), F32),
                pltpu.VMEM((n_seq, 8, cols), F32),
                pltpu.VMEM((n_head, T), F32),
                pltpu.VMEM((NX * ndp, LANES), F32),
                pltpu.VMEM((nz, LANES), F32),
                pltpu.VMEM((2, n_seq, rows, kv_width), F32),
                pltpu.VMEM((2, n_seq, rows, kv_width), BF16),
                pltpu.VMEM((2, n_seq, rows, kv_width), BF16),
                pltpu.VMEM((n_seq, rows, q_width), BF16),
                pltpu.VMEM((2, n_seq, rows, kv_width), BF16),
                pltpu.SemaphoreType.DMA((7,)),
                pltpu.SemaphoreType.DMA((n_seq + 2,)),
                pltpu.SemaphoreType.DMA((2 * n_seq,)),
                pltpu.SemaphoreType.DMA((2 * n_seq,)),
                pltpu.SemaphoreType.DMA((2,)),
                pltpu.SemaphoreType.DMA((2,)),
                pltpu.SemaphoreType.DMA((NX * ndp,)),
                pltpu.SemaphoreType.DMA((NX * ndp,)),
                pltpu.SemaphoreType.DMA((nz,)),
                pltpu.SemaphoreType.DMA((nz,)),
            ],
            compiler_params=pltpu.CompilerParams(
                collective_id=0,
                has_side_effects=True,
                vmem_limit_bytes=48 * 1024 * 1024,
            ),
        )(queries, keys, values, output_gradient, sinks, doc_starts, valid_counts)
        return outs[0], outs[1], outs[2], outs[3].reshape(n_head)

    split = P("dp", "ctx", "tp")
    return jax.shard_map(
        local,
        mesh=mesh,
        in_specs=(split, split, split, split, P("tp"), P("dp", None), P("dp", None)),
        out_specs=(split, split, split, P("tp")),
        check_vma=False,
    )
```

time: 121 us -> 61.1 us (0.50)
  the two profiles are of different devices: /device:TPU:24 before, /device:TPU:6 now
where the time goes in v1:
time: 61.1 us; the launch traced here: 60.7 us
  Pallas kernels  51.7 us (85%)
  local copies, waits for them, and re-layouts  8.33 us (14%)
  between operations  0.66 us (1%)
    pallas_call x1, Pallas kernels, local(): pl.pallas_call(functools.partial(kernel, nz, ndp, n_seq, n_head), out_sha...  51.7 us
    unnamed x18, local copies, waits for them, and re-layouts  8.33 us

profile of v1, /device:TPU:6, one launch (start us, length us, event | category | flops | bytes accessed | tf_op | source)
XLA Modules:
  0.0 60.7 jit_solution(14339951085560547101)
XLA Ops:
  0.6 0.0 copy-start
  0.6 1.0 %copy-done = bf16[2,128,1024]{2,1,0:T(8,128)(2,1)S(1)} copy-done((bf16[2,128,1024]{2,1,0:T(8,128)(2,1)S(1)}, bf16[2,128,1024]{2,1,0:T(8,128)(2,1)}, u32[]{:S(2)}) %copy-start) | copy-done | bytes 524312
  1.7 0.0 copy-start.1
  1.7 1.0 %copy-done.1 = bf16[2,128,1024]{2,1,0:T(8,128)(2,1)S(1)} copy-done((bf16[2,128,1024]{2,1,0:T(8,128)(2,1)S(1)}, bf16[2,128,1024]{2,1,0:T(8,128)(2,1)}, u32[]{:S(2)}) %copy-start.1) | copy-done | bytes 524312
  2.7 0.0 copy-start.2
  2.7 0.8 %copy-done.2 = bf16[2,128,128]{2,1,0:T(8,128)(2,1)S(1)} copy-done((bf16[2,128,128]{2,1,0:T(8,128)(2,1)S(1)}, bf16[2,128,128]{2,1,0:T(8,128)(2,1)}, u32[]{:S(2)}) %copy-start.2) | copy-done | bytes 65560
  3.6 0.0 copy-start.3
  3.6 0.8 %copy-done.3 = bf16[2,128,128]{2,1,0:T(8,128)(2,1)S(1)} copy-done((bf16[2,128,128]{2,1,0:T(8,128)(2,1)S(1)}, bf16[2,128,128]{2,1,0:T(8,128)(2,1)}, u32[]{:S(2)}) %copy-start.3) | copy-done | bytes 65560
  4.4 0.0 copy-start.4
  4.4 0.7 %copy-done.4 = s32[2,64]{1,0:T(2,128)S(1)} copy-done((s32[2,64]{1,0:T(2,128)S(1)}, s32[2,64]{1,0:T(2,128)}, u32[]{:S(2)}) %copy-start.4) | copy-done | bytes 536
  5.1 0.0 copy-start.5
  5.1 0.7 %copy-done.5 = s32[2,128]{1,0:T(2,128)S(1)} copy-done((s32[2,128]{1,0:T(2,128)S(1)}, s32[2,128]{1,0:T(2,128)}, u32[]{:S(2)}) %copy-start.5) | copy-done | bytes 1048
  5.8 0.0 copy-start.6
  5.8 0.7 %copy-done.6 = f32[16]{0:T(128)S(1)} copy-done((f32[16]{0:T(128)S(1)}, f32[16]{0:T(128)}, u32[]{:S(2)}) %copy-start.6) | copy-done | bytes 88
  6.4 51.7 %shard_map.102 = (bf16[2,128,1024]{2,1,0:T(8,128)(2,1)S(1)}, bf16[2,128,128]{2,1,0:T(8,128)(2,1)S(1)}, bf16[2,128,128]{2,1,0:T(8,128)(2,1)S(1)}, f32[1,16]{1,0:T(1,128)S(1)}) custom-call(bf16[2,128,1024]{2,1,0:T(8,128)(2,1)S(1)} %copy-done, bf16[2,128,128]{2,1,0:T(8,128)(2,1)S(1)} %copy-done.2, bf16[2,128,128]{2,1,0:T(8,128)(2,1)S(1)} %copy-done.3, ...), custom_call_target="tpu_custom_call" | custom-call | tf_op jit(solution)/shard_map/pallas_call | solution.py:334
  58.2 0.8 %copy.15 = bf16[2,128,1024]{2,1,0:T(8,128)(2,1)} copy(bf16[2,128,1024]{2,1,0:T(8,128)(2,1)S(1)} %get-tuple-element.16) | data formatting | bytes 1048576
  59.0 0.6 %copy.16 = bf16[2,128,128]{2,1,0:T(8,128)(2,1)} copy(bf16[2,128,128]{2,1,0:T(8,128)(2,1)S(1)} %get-tuple-element.17) | data formatting | bytes 131072
  59.6 0.6 %copy.17 = bf16[2,128,128]{2,1,0:T(8,128)(2,1)} copy(bf16[2,128,128]{2,1,0:T(8,128)(2,1)S(1)} %get-tuple-element.18) | data formatting | bytes 131072
  60.2 0.5 copy.18
Async XLA Ops:
  0.6 1.0 %copy-start = (bf16[2,128,1024]{2,1,0:T(8,128)(2,1)S(1)}, bf16[2,128,1024]{2,1,0:T(8,128)(2,1)}, u32[]{:S(2)}) copy-start(bf16[2,128,1024]{2,1,0:T(8,128)(2,1)} %q_hbm.1) | copy-start | bytes 1572868
  1.7 1.0 %copy-start.1 = (bf16[2,128,1024]{2,1,0:T(8,128)(2,1)S(1)}, bf16[2,128,1024]{2,1,0:T(8,128)(2,1)}, u32[]{:S(2)}) copy-start(bf16[2,128,1024]{2,1,0:T(8,128)(2,1)} %g_hbm.1) | copy-start | bytes 1572868
  2.7 0.8 %copy-start.2 = (bf16[2,128,128]{2,1,0:T(8,128)(2,1)S(1)}, bf16[2,128,128]{2,1,0:T(8,128)(2,1)}, u32[]{:S(2)}) copy-start(bf16[2,128,128]{2,1,0:T(8,128)(2,1)} %k_hbm.1) | copy-start | bytes 196612
  3.6 0.8 %copy-start.3 = (bf16[2,128,128]{2,1,0:T(8,128)(2,1)S(1)}, bf16[2,128,128]{2,1,0:T(8,128)(2,1)}, u32[]{:S(2)}) copy-start(bf16[2,128,128]{2,1,0:T(8,128)(2,1)} %v_hbm.1) | copy-start | bytes 196612
  4.4 0.7 %copy-start.4 = (s32[2,64]{1,0:T(2,128)S(1)}, s32[2,64]{1,0:T(2,128)}, u32[]{:S(2)}) copy-start(s32[2,64]{1,0:T(2,128)} %starts_hbm.1) | copy-start | bytes 1540
  5.1 0.7 %copy-start.5 = (s32[2,128]{1,0:T(2,128)S(1)}, s32[2,128]{1,0:T(2,128)}, u32[]{:S(2)}) copy-start(s32[2,128]{1,0:T(2,128)} %counts_hbm.1) | copy-start | bytes 3076
  5.8 0.7 %copy-start.6 = (f32[16]{0:T(128)S(1)}, f32[16]{0:T(128)}, u32[]{:S(2)}) copy-start(f32[16]{0:T(128)} %sinks_hbm.1) | copy-start | bytes 196

commit v2 on v1

--- a/solution.py
+++ b/solution.py
@@ -15,6 +15,7 @@
 LANES = 128
 LOG2E = 1.4426950408889634
 MASKED = -1e30
+JUMP = 8
 NX = 4
 
 
@@ -68,10 +69,7 @@
     dkv_own,
     dkv_send,
     dkv_recv,
-    dq_v,
-    dkv_v,
     in_sem,
-    out_sem,
     halo_send,
     halo_recv,
     grad_send,
@@ -80,6 +78,9 @@
     plane_recv,
     ring_send,
     ring_recv,
+    know_1,
+    know_2,
+    know_4,
 ):
     n_ctx = nz * NX
     ctx = lax.axis_index("ctx")
@@ -96,15 +97,14 @@
         return {"ctx": z * NX + other % NX, "dp": other // NX}
 
     def ring_peer(k):
-        return {"ctx": ((z + k) % nz) * NX + x}
-
-    barrier = pltpu.get_barrier_semaphore()
-    pl.semaphore_signal(barrier, inc=1, device_id={"ctx": left}, device_id_type=MESH)
-    pl.semaphore_signal(barrier, inc=1, device_id={"ctx": right}, device_id_type=MESH)
-    for k in range(1, n_plane):
-        pl.semaphore_signal(barrier, inc=1, device_id=plane_peer(k), device_id_type=MESH)
-    for k in range(1, nz):
-        pl.semaphore_signal(barrier, inc=1, device_id=ring_peer(k), device_id_type=MESH)
+        return {"ctx": ((z + k + nz) % nz) * NX + x}
+
+    def x_peer(k):
+        return {"ctx": z * NX + (x + k) % NX}
+
+    def greet(sem, peers):
+        for peer in peers:
+            pl.semaphore_signal(sem, inc=1, device_id=peer, device_id_type=MESH)
 
     loads = [
         pltpu.make_async_copy(k_hbm, kv_own.at[0], in_sem.at[0]),
@@ -115,11 +115,17 @@
         pltpu.make_async_copy(q_hbm, q, in_sem.at[5]),
         pltpu.make_async_copy(g_hbm, g, in_sem.at[6]),
     ]
-    for copy in loads:
+    loads[0].start()
+    loads[1].start()
+    barrier = pltpu.get_barrier_semaphore()
+    near = [x_peer(1), x_peer(NX - 1), ring_peer(1), ring_peer(-1)]
+    near += [{"dp": (dp + k) % ndp} for k in range(1, ndp)]
+    greet(barrier, [{"ctx": right}, {"ctx": left}] + near)
+    for copy in loads[2:]:
         copy.start()
     loads[0].wait()
     loads[1].wait()
-    pl.semaphore_wait(barrier, 2 + (n_plane - 1) + (nz - 1))
+    pl.semaphore_wait(barrier, 2 + len(near))
 
     halos = []
     for b in range(n_seq):
@@ -134,6 +140,7 @@
             )
             copy.start()
             halos.append(copy)
+    greet(know_1, near)
 
     key_row = lax.broadcasted_iota(jnp.int32, (T, T), 0)
     query_col = lax.broadcasted_iota(jnp.int32, (T, T), 1)
@@ -181,11 +188,19 @@
             s_own[b, :, cols] = nt(kv_own[0, b], qs[b, cols, :])
             p_own[b, :, cols] = nt(kv_own[1, b], gs[b, cols, :])
 
+    pl.semaphore_wait(know_1, len(near))
+    next_2 = [x_peer(2), ring_peer(2), ring_peer(-2)]
+    greet(know_2, next_2)
+
     scale = D**-0.5
     own2 = lax.broadcasted_iota(jnp.int32, (T, W), 0) <= (
         lax.broadcasted_iota(jnp.int32, (T, W), 1) % T
     )
     for b in range(n_seq):
+        if b == 1:
+            pl.semaphore_wait(know_2, len(next_2))
+            next_4 = [ring_peer(4), ring_peer(-4)]
+            greet(know_4, next_4)
         halos[2 * b].wait_recv()
         halos[2 * b + 1].wait_recv()
         for c in range(n_chunk):
@@ -238,9 +253,7 @@
         copy.start()
         plane_copies.append(copy)
 
-    ring_copies = []
     grad_copies = []
-    out_copies = []
 
     def backward(b):
         k_all = jnp.concatenate([kv_own[0, b], kv_prev[0, b]], axis=0)
@@ -266,34 +279,37 @@
             kv = 0 if 2 * c < heads_per_kv else 1
             part = dqt[kv * D : (kv + 1) * D, :]
             pair = jnp.concatenate([part[:, :T], part[:, T:]], axis=0)
-            dq_v[b, :, c * LANES : (c + 1) * LANES] = (pair.T * scale).astype(BF16)
+            dq_out[b, :, c * LANES : (c + 1) * LANES] = (pair.T * scale).astype(BF16)
         dk = dk * scale
         dkv_own[0, b] = dk[:T]
         dkv_own[1, b] = dv[:T]
         dkv_send[0, b] = dk[T:].astype(BF16)
         dkv_send[1, b] = dv[T:].astype(BF16)
-        copy = pltpu.make_async_copy(dq_v.at[b], dq_out.at[b], out_sem.at[b])
-        copy.start()
-        out_copies.append(copy)
-
-    backward(0)
+
+    for b in range(n_seq):
+        backward(b)
     for copy in plane_copies:
         copy.wait_recv()
     ring[pl.ds(z, 1), :] = jnp.sum(plane[...], axis=0, keepdims=True)
-    order = sorted(range(1, nz), key=lambda k: -min(k, nz - k))
-    for k in order:
+    pl.semaphore_wait(know_4, len(next_4))
+
+    def send_row(k, to, sems):
+        at = pl.ds((z + k + nz) % nz, 1)
         copy = pltpu.make_async_remote_copy(
-            src_ref=ring.at[pl.ds(z, 1)],
-            dst_ref=ring.at[pl.ds(z, 1)],
-            send_sem=ring_send.at[k],
-            recv_sem=ring_recv.at[k],
-            device_id=ring_peer(k),
+            src_ref=ring.at[at],
+            dst_ref=ring.at[at],
+            send_sem=sems[0],
+            recv_sem=sems[1],
+            device_id=ring_peer(to),
             device_id_type=MESH,
         )
         copy.start()
-        ring_copies.append(copy)
-    for b in range(1, n_seq):
-        backward(b)
+        return copy
+
+    up, down, far_up, far_down = {}, {}, {}, {}
+    for k in range(JUMP, 0, -1):
+        up[k] = send_row(0, k, (ring_send.at[k], ring_recv.at[k]))
+        down[k] = send_row(0, -k, (ring_send.at[JUMP + k], ring_recv.at[JUMP + k]))
     for t in range(2):
         copy = pltpu.make_async_remote_copy(
             src_ref=dkv_send.at[t],
@@ -305,20 +321,34 @@
         )
         copy.start()
         grad_copies.append(copy)
+    for k in range(1, JUMP + 1):
+        down[k].wait_recv()
+        i = 2 * JUMP + k
+        far_down[k] = send_row(k, -JUMP, (ring_send.at[i], ring_recv.at[i]))
+        up[k].wait_recv()
+        if k < JUMP:
+            i = 3 * JUMP + k
+            far_up[k] = send_row(-k, JUMP, (ring_send.at[i], ring_recv.at[i]))
+    far_copies = list(far_down.values()) + list(far_up.values())
+    ring_copies = list(up.values()) + list(down.values()) + far_copies
     not_last = jnp.where(ctx < n_ctx - 1, 1.0, 0.0)
     for t, out in ((0, dk_out), (1, dv_out)):
         grad_copies[t].wait_recv()
-        dkv_v[t] = (dkv_own[t] + dkv_recv[t].astype(F32) * not_last).astype(BF16)
-        copy = pltpu.make_async_copy(dkv_v.at[t], out, out_sem.at[n_seq + t])
-        copy.start()
-        out_copies.append(copy)
+        out[...] = (dkv_own[t] + dkv_recv[t].astype(F32) * not_last).astype(BF16)
     for copy in halos + plane_copies + ring_copies + grad_copies:
         copy.wait_send()
-    for copy in out_copies:
-        copy.wait()
-    for copy in ring_copies:
+    for copy in far_copies:
         copy.wait_recv()
     sink_out[...] = -jnp.sum(ring[...], axis=0, keepdims=True)[:, :n_head]
+
+
+def write_out(dq, dk, dv, sink, dq_hbm, dk_hbm, dv_hbm, sink_hbm, sem):
+    pairs = ((dq, dq_hbm), (dk, dk_hbm), (dv, dv_hbm), (sink, sink_hbm))
+    copies = [pltpu.make_async_copy(src, dst, sem.at[i]) for i, (src, dst) in enumerate(pairs)]
+    for copy in copies:
+        copy.start()
+    for copy in copies:
+        copy.wait()
 
 
 def solution(mesh):
@@ -329,23 +359,19 @@
         n_seq, rows, q_width = queries.shape
         n_head = sinks.shape[0]
         kv_width = keys.shape[2]
-        any_space = pl.BlockSpec(memory_space=pl.ANY)
+        hbm = pl.BlockSpec(memory_space=pltpu.HBM)
+        vmem = pl.BlockSpec(memory_space=pltpu.VMEM)
         cols = n_head * T
         outs = pl.pallas_call(
             functools.partial(kernel, nz, ndp, n_seq, n_head),
             out_shape=(
-                jax.ShapeDtypeStruct(queries.shape, BF16),
-                jax.ShapeDtypeStruct(keys.shape, BF16),
-                jax.ShapeDtypeStruct(values.shape, BF16),
-                jax.ShapeDtypeStruct((1, n_head), F32),
+                pltpu.VMEM(queries.shape, BF16),
+                pltpu.VMEM(keys.shape, BF16),
+                pltpu.VMEM(values.shape, BF16),
+                pltpu.VMEM((1, n_head), F32),
             ),
-            in_specs=[any_space] * 7,
-            out_specs=(
-                any_space,
-                any_space,
-                any_space,
-                pl.BlockSpec(memory_space=pltpu.VMEM),
-            ),
+            in_specs=[hbm] * 7,
+            out_specs=(vmem,) * 4,
             scratch_shapes=[
                 pltpu.VMEM((n_seq, rows, q_width), BF16),
                 pltpu.VMEM((n_seq, rows, q_width), BF16),
@@ -369,25 +395,38 @@
                 pltpu.VMEM((2, n_seq, rows, kv_width), F32),
                 pltpu.VMEM((2, n_seq, rows, kv_width), BF16),
                 pltpu.VMEM((2, n_seq, rows, kv_width), BF16),
-                pltpu.VMEM((n_seq, rows, q_width), BF16),
-                pltpu.VMEM((2, n_seq, rows, kv_width), BF16),
                 pltpu.SemaphoreType.DMA((7,)),
-                pltpu.SemaphoreType.DMA((n_seq + 2,)),
                 pltpu.SemaphoreType.DMA((2 * n_seq,)),
                 pltpu.SemaphoreType.DMA((2 * n_seq,)),
                 pltpu.SemaphoreType.DMA((2,)),
                 pltpu.SemaphoreType.DMA((2,)),
                 pltpu.SemaphoreType.DMA((NX * ndp,)),
                 pltpu.SemaphoreType.DMA((NX * ndp,)),
-                pltpu.SemaphoreType.DMA((nz,)),
-                pltpu.SemaphoreType.DMA((nz,)),
+                pltpu.SemaphoreType.DMA((4 * JUMP + 1,)),
+                pltpu.SemaphoreType.DMA((4 * JUMP + 1,)),
+                pltpu.SemaphoreType.REGULAR,
+                pltpu.SemaphoreType.REGULAR,
+                pltpu.SemaphoreType.REGULAR,
             ],
             compiler_params=pltpu.CompilerParams(
                 collective_id=0,
                 has_side_effects=True,
                 vmem_limit_bytes=48 * 1024 * 1024,
             ),
-        )(queries, keys, values, output_gradient, sinks, doc_starts, valid_counts)
+        )(*[pltpu.with_memory_space_constraint(a, pltpu.HBM) for a in (queries, keys, values, output_gradient, sinks, doc_starts, valid_counts)])
+        outs = pl.pallas_call(
+            write_out,
+            out_shape=(
+                jax.ShapeDtypeStruct(queries.shape, BF16),
+                jax.ShapeDtypeStruct(keys.shape, BF16),
+                jax.ShapeDtypeStruct(values.shape, BF16),
+                jax.ShapeDtypeStruct((1, n_head), F32),
+            ),
+            in_specs=[vmem] * 4,
+            out_specs=(hbm,) * 4,
+            scratch_shapes=[pltpu.SemaphoreType.DMA((4,))],
+            compiler_params=pltpu.CompilerParams(vmem_limit_bytes=1024 * 1024),
+        )(*outs)
         return outs[0], outs[1], outs[2], outs[3].reshape(n_head)
 
     split = P("dp", "ctx", "tp")

time: 61.1 us -> 48.3 us (0.79)
  the two profiles are of different devices: /device:TPU:6 before, /device:TPU:2 now
where the time goes in v2:
time: 48.3 us; the launch traced here: 48.1 us
  Pallas kernels  47.5 us (98%)
  between operations  0.64 us (1%)
    pallas_call x1, Pallas kernels, local(): pl.pallas_call(functools.partial(kernel, nz, ndp, n_seq, n_head), out_sha...  46.6 us

profile of v2, /device:TPU:2, one launch (start us, length us, event | category | flops | bytes accessed | tf_op | source)
XLA Modules:
  0.0 48.1 jit_solution(8485670716392604287)
XLA Ops:
  0.6 46.6 %shard_map.102 = (bf16[2,128,1024]{2,1,0:T(8,128)(2,1)S(1)}, bf16[2,128,128]{2,1,0:T(8,128)(2,1)S(1)}, bf16[2,128,128]{2,1,0:T(8,128)(2,1)S(1)}, f32[1,16]{1,0:T(1,128)S(1)}) custom-call(bf16[2,128,1024]{2,1,0:T(8,128)(2,1)} %q_hbm.1, bf16[2,128,128]{2,1,0:T(8,128)(2,1)} %k_hbm.1, bf16[2,128,128]{2,1,0:T(8,128)(2,1)} %v_hbm.1, bf16[2,128,1024]{2,1,0:T(8,128)(2,1)} %g_hbm.1, ...), custom_call_target="tpu_custom_call" | custom-call | tf_op jit(solution)/shard_map/pallas_call | solution.py:365
  47.3 0.9 %shard_map.103 = (bf16[2,128,1024]{2,1,0:T(8,128)(2,1)}, bf16[2,128,128]{2,1,0:T(8,128)(2,1)}, bf16[2,128,128]{2,1,0:T(8,128)(2,1)}, f32[1,16]{1,0:T(1,128)}) custom-call(bf16[2,128,1024]{2,1,0:T(8,128)(2,1)S(1)} %get-tuple-element.12.dq, bf16[2,128,128]{2,1,0:T(8,128)(2,1)S(1)} %get-tuple-element.13.dk, bf16[2,128,128]{2,1,0:T(8,128)(2,1)S(1)} %get-tuple-element.14.dv, ...), custom_call_target="tpu_custom_call" | custom-call | tf_op jit(solution)/shard_map/pallas_call | solution.py:417
